TPU v7x, 32 devices: a whole 2x2x4 slice. The times are simulated.
32 devices in a mesh: band: 8 (over z, x), plane: 4 (over y, core).
Axes of the slice: x: 2, y: 2, z: 4, core: 2. Of those that a mesh axis runs over, the one named last changes fastest.
Arguments:
- orbitals: float32 [8, 112, 12544], P('band', 'plane'), may hold values from -6 to 6
Outputs:
- exchange_w: float32 [8, 112, 12544], P('band', 'plane')
All inputs are finite; a program needn't handle non-finite values.
Results may differ from a plain program's by a relative error of at most 0.000082.
Values sent between devices are 32-bit elements; how exact they have to be, the bound alone decides.
A program may use at most 64 MiB of HBM per device.

v0:
```python
import functools
import math

import jax
import jax.numpy as jnp
import numpy as np
from jax import lax
from jax.experimental import pallas as pl
from jax.experimental.pallas import tpu as pltpu
from jax.sharding import PartitionSpec as P

SOURCES = 2

screen_omega = 0.106
cell_length = 46.93
mixing = 0.25
high = lax.Precision.HIGH


def kernel_values(squares):
    gsquare = squares * (2.0 * math.pi / cell_length) ** 2
    safe = jnp.where(gsquare > 0, gsquare, 1.0)
    values = 4.0 * math.pi / safe * (1.0 - jnp.exp(-safe / (4.0 * screen_omega * screen_omega)))
    return jnp.where(gsquare > 0, values, math.pi / (screen_omega * screen_omega))


def real_basis(count):
    half = count // 2
    freq = np.array(list(range(half + 1)) + list(range(1, count - half)))
    angle = 2.0 * np.pi * (np.arange(count)[:, None] * freq[None, :] % count) / count
    table = np.where(np.arange(count)[None, :] <= half, np.cos(angle), np.sin(angle))
    table = table / np.sqrt((table**2).sum(axis=0, keepdims=True))
    return table.astype(np.float32), freq.astype(np.float32)


def spread_kernel(nband, chunks, psi_ref, src_ref, send_sem, recv_sem, own_sem):
    me = lax.axis_index("band")
    mine = lax.rem(me, SOURCES)
    partner = me + 1 - 2 * mine
    above = lax.rem(me + 2, nband)
    below = lax.rem(me + nband - 2, nband)
    size = psi_ref.shape[0] // chunks

    barrier = pltpu.get_barrier_semaphore()
    for other in (partner, above, below):
        pl.semaphore_signal(barrier, inc=1, device_id={"band": other}, device_id_type=pl.DeviceIdType.MESH)
    pl.semaphore_wait(barrier, 3)

    def part(which, c):
        return src_ref.at[which, pl.ds(c * size, size)]

    def own(c):
        return pltpu.make_async_copy(psi_ref.at[pl.ds(c * size, size)], part(mine, c), own_sem.at[c])

    def remote(kind, which, c, target):
        return pltpu.make_async_remote_copy(
            src_ref=part(which, c),
            dst_ref=part(which, c),
            send_sem=send_sem.at[kind, c],
            recv_sem=recv_sem.at[kind, c],
            device_id={"band": target},
            device_id_type=pl.DeviceIdType.MESH,
        )

    @pl.when(me < SOURCES)
    def _():
        for c in range(chunks):
            own(c).start()

    for c in range(chunks):
        @pl.when(me < SOURCES)
        def _():
            own(c).wait()

        @pl.when(me >= SOURCES)
        def _():
            remote(0, mine, c, above).wait_recv()

        @pl.when(me + 2 < nband)
        def _():
            remote(0, mine, c, above).start()

        remote(1, mine, c, partner).start()

    for c in range(chunks):
        remote(1, 1 - mine, c, partner).wait_recv()
        remote(1, mine, c, partner).wait_send()

        @pl.when(me + 2 < nband)
        def _():
            remote(0, mine, c, above).wait_send()


def spread(local):
    nband = lax.axis_size("band")
    thick = local.shape[0]
    chunks = next(c for c in (14, 7, 1) if thick % c == 0)
    return pl.pallas_call(
        functools.partial(spread_kernel, nband, chunks),
        out_shape=jax.ShapeDtypeStruct((SOURCES,) + local.shape, jnp.float32),
        in_specs=[pl.BlockSpec(memory_space=pltpu.VMEM)],
        out_specs=pl.BlockSpec(memory_space=pltpu.VMEM),
        scratch_shapes=[
            pltpu.SemaphoreType.DMA((2, chunks)),
            pltpu.SemaphoreType.DMA((2, chunks)),
            pltpu.SemaphoreType.DMA((chunks,)),
        ],
        compiler_params=pltpu.CompilerParams(collective_id=0, has_side_effects=True),
        name="spread",
    )(local)


def on_device(orbitals):
    nplane = lax.axis_size("plane")
    rows, thick, flat = orbitals.shape
    count = thick * nplane
    table, freq = real_basis(count)
    freq = jnp.asarray(freq)
    local = orbitals.reshape(rows * thick, count, count)
    freq_mine = lax.dynamic_slice(freq, (lax.axis_index("plane") * thick,), (thick,))
    kernel = kernel_values(
        freq[:, None, None] ** 2 + freq_mine[None, :, None] ** 2 + freq[None, None, :] ** 2
    )
    sources = spread(local)

    def along(spec, values):
        return jnp.einsum(spec, values, table, precision=high)

    total = 0.0
    for j in range(SOURCES):
        density = local * sources[j]
        spectrum = along("xbc,yb->xyc".replace("yb", "by"), along("xyz,zc->xyc", density))
        moved = lax.all_to_all(spectrum, "plane", split_axis=1, concat_axis=0, tiled=True)
        filtered = along("xbc,xa->abc", moved) * kernel
        back = along("abc,xa->xbc", filtered)
        back = lax.all_to_all(back, "plane", split_axis=0, concat_axis=1, tiled=True)
        potential = along("xyc,zc->xyz", along("xbc,yb->xyc", back))
        total = total + sources[j] * potential
    return (-mixing * total).reshape(rows, thick, flat)


def solution(mesh):
    placed = (P("band", "plane", None),)
    return jax.shard_map(
        on_device, mesh=mesh, in_specs=placed, out_specs=P("band", "plane", None), check_vma=False
    )
```

profile of v0, /device:TPU:25, one launch (start us, length us, event | category | flops | bytes accessed | tf_op | source)
XLA Modules:
  0.0 188.2 jit_solution(10675798983696909)
XLA Ops:
  0.0 4.7 %reduce = f32[28,12544]{1,0:T(8,128)S(1)} reduce(f32[1,28,12544]{2,0,1:T(1,128)} %param.14, f32[]{:T(128)} %constant.39), dimensions={0}, to_apply=%param.14.reduce_sub_computation | reduce | bytes 2809860 | tf_op args[0]
  4.7 2.6 %reshape.42.psi_ref = f32[28,112,112]{2,1,0:T(8,128)} reshape(f32[28,12544]{1,0:T(8,128)S(1)} %reduce) | data formatting | bytes 2809856 | tf_op jit(solution)/shard_map/reshape | solution.py:119
  7.3 54.0 %spread.1 = f32[2,28,112,112]{3,2,1,0:T(8,128)} custom-call(f32[28,112,112]{2,1,0:T(8,128)} %reshape.42.psi_ref), custom_call_target="tpu_custom_call" | custom-call | tf_op jit(solution)/shard_map/spread/pallas_call | solution.py:98
  61.3 0.0 copy-done
  61.3 0.0 copy-done.2
  61.3 3.2 %fusion.2 = f32[28,112,112]{1,2,0:T(8,128)S(1)} fusion(f32[112,112,1]{1,0,2:T(8,128)S(1)} %copy-done.2, f32[28,112,112]{2,1,0:T(8,128)S(1)} %copy-done, f32[2,28,112,112]{3,2,1,0:T(8,128)} %spread.1), kind=kOutput, calls=%fused_computation.6 | convolution fusion | flops 236379136 | bytes 4465664 | tf_op jit(solution)/shard_map/xyz,zc->xyc/dot_general | solution.py:127
  64.5 0.8 convolution_bitcast_fusion
  65.3 2.3 %copy.31 = f32[28,112,112]{2,0,1:T(8,128)} copy(f32[28,112,112]{1,2,0:T(8,128)S(1)} %convolution_bitcast_fusion) | data formatting | bytes 2809856 | tf_op jit(solution)/shard_map/xbc,by->xyc/transpose | solution.py:127
  67.5 6.7 %all-to-all-start.2 = ((f32[28,112,112]{2,0,1:T(8,128)}), f32[28,112,112]{2,0,1:T(8,128)S(1)}, u32[]{:S(2)}, u32[]{:S(2)}) async-start(f32[28,112,112]{2,0,1:T(8,128)} %copy.31), calls=%async_computation.2 | async-start | bytes 3670016 | tf_op jit(solution)/shard_map/all_to_all | solution.py:133
  74.2 3.2 %fusion.7 = f32[28,112,112]{1,2,0:T(8,128)S(1)} fusion(f32[112,112,1]{1,0,2:T(8,128)S(1)} %copy-done.2, f32[28,112,112]{2,1,0:T(8,128)S(1)} %copy-done, f32[2,28,112,112]{3,2,1,0:T(8,128)} %spread.1), kind=kOutput, calls=%fused_computation.13 | convolution fusion | flops 236379136 | bytes 4465664 | tf_op jit(solution)/shard_map/xyz,zc->xyc/dot_general | solution.py:127
  77.4 0.8 convolution_bitcast_fusion.1
  78.2 2.3 %copy.22 = f32[28,112,112]{2,0,1:T(8,128)} copy(f32[28,112,112]{1,2,0:T(8,128)S(1)} %convolution_bitcast_fusion.1) | data formatting | bytes 2809856 | tf_op jit(solution)/shard_map/xbc,by->xyc/transpose | solution.py:127
  80.6 15.6 %all-to-all-done.2 = f32[28,112,112]{2,0,1:T(8,128)S(1)} async-done(((f32[28,112,112]{2,0,1:T(8,128)}), f32[28,112,112]{2,0,1:T(8,128)S(1)}, u32[]{:S(2)}, u32[]{:S(2)}) %all-to-all-start.2) | async-done | bytes 1404960 | tf_op jit(solution)/shard_map/all_to_all | solution.py:133
  96.1 5.3 %all-to-all-start = ((f32[28,112,112]{2,0,1:T(8,128)}), f32[28,112,112]{2,0,1:T(8,128)}, u32[]{:S(2)}, u32[]{:S(2)}) async-start(f32[28,112,112]{2,0,1:T(8,128)} %copy.22), calls=%async_computation | async-start | bytes 3670016 | tf_op jit(solution)/shard_map/all_to_all | solution.py:133
  101.5 0.0 copy-done.9
  101.5 0.1 dynamic-slice_multiply_fusion
  101.5 0.0 copy-done.6
  101.5 0.7 broadcast_add_fusion
  102.2 0.9 copy.32
  103.2 0.0 copy-start.3
  103.2 0.1 reshape.47
  103.3 0.7 copy-done.3
  104.0 1.7 fusion.8
  105.6 0.0 copy-done.4
  105.7 0.0 copy-done.7
  105.7 1.8 fusion.12
  107.5 1.8 copy.34
  109.2 14.2 %all-to-all-done = f32[28,112,112]{2,0,1:T(8,128)} async-done(((f32[28,112,112]{2,0,1:T(8,128)}), f32[28,112,112]{2,0,1:T(8,128)}, u32[]{:S(2)}, u32[]{:S(2)}) %all-to-all-start) | async-done | bytes 1404960 | tf_op jit(solution)/shard_map/all_to_all | solution.py:133
  123.5 4.5 %all-to-all-start.3 = ((f32[112,28,112]{2,1,0:T(8,128)}), f32[112,28,112]{2,1,0:T(8,128)S(1)}, u32[]{:S(2)}, u32[]{:S(2)}) async-start(f32[112,28,112]{2,1,0:T(8,128)} %copy.34), calls=%async_computation.3 | async-start | bytes 3670016 | tf_op jit(solution)/shard_map/all_to_all | solution.py:136
  128.0 2.4 %copy.23 = f32[28,112,112]{2,1,0:T(8,128)S(1)} copy(f32[28,112,112]{2,0,1:T(8,128)} %all-to-all-done) | data formatting | bytes 2809856 | tf_op jit(solution)/shard_map/all_to_all | solution.py:133
  130.4 1.4 reshape.44
  131.8 3.2 %fusion.10 = f32[112,28,112]{2,0,1:T(8,128)S(1)} fusion(f32[112,112,1]{0,1,2:T(8,128)S(1)} %copy-done.3, f32[112,28,112]{2,1,0:T(8,128)} %reshape.44), kind=kOutput, calls=%fused_computation.16 | convolution fusion | flops 236027904 | bytes 2860032 | tf_op jit(solution)/shard_map/xbc,xa->abc/dot_general | solution.py:127
  135.0 0.0 copy-done.5
  135.0 0.0 copy-done.8
  135.0 1.8 fusion.14
  136.8 1.8 copy.25
  138.6 11.3 %all-to-all-done.3 = f32[112,28,112]{2,1,0:T(8,128)S(1)} async-done(((f32[112,28,112]{2,1,0:T(8,128)}), f32[112,28,112]{2,1,0:T(8,128)S(1)}, u32[]{:S(2)}, u32[]{:S(2)}) %all-to-all-start.3) | async-done | bytes 1404960 | tf_op jit(solution)/shard_map/all_to_all | solution.py:136
  149.9 5.3 %all-to-all-start.1 = ((f32[112,28,112]{2,1,0:T(8,128)}), f32[112,28,112]{2,1,0:T(8,128)}, u32[]{:S(2)}, u32[]{:S(2)}) async-start(f32[112,28,112]{2,1,0:T(8,128)} %copy.25), calls=%async_computation.1 | async-start | bytes 3670016 | tf_op jit(solution)/shard_map/all_to_all | solution.py:136
  155.2 1.5 copy.36
  156.7 1.5 all_to_all.67
  158.2 1.4 fusion.33
  159.7 1.4 fusion
  161.1 16.1 %all-to-all-done.1 = f32[112,28,112]{2,1,0:T(8,128)} async-done(((f32[112,28,112]{2,1,0:T(8,128)}), f32[112,28,112]{2,1,0:T(8,128)}, u32[]{:S(2)}, u32[]{:S(2)}) %all-to-all-start.1) | async-done | bytes 1404960 | tf_op jit(solution)/shard_map/all_to_all | solution.py:136
  177.2 1.7 copy.27
  178.9 1.3 all_to_all.59
  180.2 3.0 %fusion.32 = f32[28,112,112]{2,1,0:T(8,128)S(1)} fusion(f32[28,112,112]{2,1,0:T(8,128)} %all_to_all.59, f32[112,112,1]{1,0,2:T(8,128)S(1)} %copy-done.2), kind=kOutput, calls=%fused_computation.40 | convolution fusion | flops 236027904 | bytes 2860032 | tf_op jit(solution)/shard_map/xbc,yb->xyc/dot_general | solution.py:127
  183.2 1.5 fusion.4
  184.7 3.5 %reshape.54 = f32[1,28,12544]{2,0,1:T(1,128)} reshape(f32[28,112,112]{2,1,0:T(8,128)S(1)} %fusion.4) | data formatting | bytes 2809856 | tf_op jit(solution)/shard_map/reshape | solution.py:139
  (10 shorter events, 0.0 us)
Async XLA Ops:
  7.3 54.0 %copy-start = (f32[28,112,112]{2,1,0:T(8,128)S(1)}, f32[28,112,112]{2,1,0:T(8,128)}, u32[]{:S(2)}) copy-start(f32[28,112,112]{2,1,0:T(8,128)} %reshape.42.psi_ref) | copy-start | bytes 4214788
  7.3 54.0 %copy-start.2 = (f32[112,112,1]{1,0,2:T(8,128)S(1)}, f32[112,112,1]{1,0,2:T(8,128)}, u32[]{:S(2)}) copy-start(f32[112,112,1]{1,0,2:T(8,128)} %constant.37) | copy-start | bytes 150532
  67.5 28.6 %all-to-all-start.2 = ((f32[28,112,112]{2,0,1:T(8,128)}), f32[28,112,112]{2,0,1:T(8,128)S(1)}, u32[]{:S(2)}, u32[]{:S(2)}) async-start(f32[28,112,112]{2,0,1:T(8,128)} %copy.31), calls=%async_computation.2 | async-start | bytes 3670016 | tf_op jit(solution)/shard_map/all_to_all | solution.py:133
  80.6 20.9 %copy-start.9 = (f32[112]{0:T(128)S(1)}, f32[112]{0:T(128)}, u32[]{:S(2)}) copy-start(f32[112]{0:T(128)} %constant.30.clone) | copy-start | bytes 1348
  80.6 21.0 %copy-start.6 = (f32[112]{0:T(128)S(1)}, f32[112]{0:T(128)}, u32[]{:S(2)}) copy-start(f32[112]{0:T(128)} %constant.36) | copy-start | bytes 1348
  96.1 27.3 %all-to-all-start = ((f32[28,112,112]{2,0,1:T(8,128)}), f32[28,112,112]{2,0,1:T(8,128)}, u32[]{:S(2)}, u32[]{:S(2)}) async-start(f32[28,112,112]{2,0,1:T(8,128)} %copy.22), calls=%async_computation | async-start | bytes 3670016 | tf_op jit(solution)/shard_map/all_to_all | solution.py:133
  103.2 0.8 copy-start.3
  104.0 1.7 copy-start.4
  104.0 1.7 copy-start.7
  123.5 26.4 %all-to-all-start.3 = ((f32[112,28,112]{2,1,0:T(8,128)}), f32[112,28,112]{2,1,0:T(8,128)S(1)}, u32[]{:S(2)}, u32[]{:S(2)}) async-start(f32[112,28,112]{2,1,0:T(8,128)} %copy.34), calls=%async_computation.3 | async-start | bytes 3670016 | tf_op jit(solution)/shard_map/all_to_all | solution.py:136
  131.8 3.2 %copy-start.5 = (f32[112,28]{0,1:T(8,128)S(1)}, f32[112,28]{0,1:T(8,128)}, u32[]{:S(2)}) copy-start(f32[112,28]{0,1:T(8,128)} %broadcast_add_fusion) | copy-start | bytes 37636
  131.8 3.2 %copy-start.8 = (f32[112]{0:T(128)S(1)}, f32[112]{0:T(128)}, u32[]{:S(2)}) copy-start(f32[112]{0:T(128)} %constant.36) | copy-start | bytes 1348
  149.9 27.3 %all-to-all-start.1 = ((f32[112,28,112]{2,1,0:T(8,128)}), f32[112,28,112]{2,1,0:T(8,128)}, u32[]{:S(2)}, u32[]{:S(2)}) async-start(f32[112,28,112]{2,1,0:T(8,128)} %copy.25), calls=%async_computation.1 | async-start | bytes 3670016 | tf_op jit(solution)/shard_map/all_to_all | solution.py:136
  180.2 3.0 %copy-start.1 = (f32[2,28,112,112]{3,2,1,0:T(8,128)S(1)}, f32[2,28,112,112]{3,2,1,0:T(8,128)}, u32[]{:S(2)}) copy-start(f32[2,28,112,112]{3,2,1,0:T(8,128)} %spread.1) | copy-start | bytes 8429572
where the time goes:
time: 189 us; the launch traced here: 188 us
  waiting for transfers between devices  57.2 us (30%)
  Pallas kernels  54 us (29%)
  local copies, waits for them, and re-layouts  25.8 us (14%)
  matrix products  23.7 us (13%)
  starting transfers between devices  21.9 us (12%)
  other arithmetic  5.45 us (3%)
    pallas_call x1, Pallas kernels, spread(): pl.pallas_call(functools.partial(spread_kernel, nband, chunks), out_shape...  54 us
    all_to_all x2, waiting for transfers between devices, on_device(): lax.all_to_all(spectrum, 'plane', split_axis=1, concat_axis=0, tiled=True)  29.8 us
    all_to_all x2, waiting for transfers between devices, on_device(): lax.all_to_all(back, 'plane', split_axis=0, concat_axis=1, tiled=True)  27.4 us
    dot_general x12, matrix products, along(): return jnp.einsum(spec, values, table, precision=high)  23.7 us
    all_to_all x2, starting transfers between devices, on_device(): lax.all_to_all(spectrum, 'plane', split_axis=1, concat_axis=0, tiled=True)  12 us
    all_to_all x2, starting transfers between devices, on_device(): lax.all_to_all(back, 'plane', split_axis=0, concat_axis=1, tiled=True)  9.85 us
    all_to_all x4, local copies, waits for them, and re-layouts, on_device(): lax.all_to_all(back, 'plane', split_axis=0, concat_axis=1, tiled=True)  6.01 us
    dot_general x4, local copies, waits for them, and re-layouts, along(): return jnp.einsum(spec, values, table, precision=high)  5.06 us
  transfers between devices with their start and end apart: 4, of which 4 were waited for; matrix products, arithmetic and copies ran while one was open for 15% of the time, Pallas kernels for 0%

commit v1 on v0

v1 whole, which is shorter than its diff:
```python
import functools
import math

import jax
import jax.numpy as jnp
import numpy as np
from jax import lax
from jax.experimental import pallas as pl
from jax.experimental.pallas import tpu as pltpu
from jax.sharding import PartitionSpec as P

SOURCES = 2

screen_omega = 0.106
cell_length = 46.93
mixing = 0.25


def kernel_values(squares):
    gsquare = squares * (2.0 * math.pi / cell_length) ** 2
    safe = jnp.where(gsquare > 0, gsquare, 1.0)
    values = 4.0 * math.pi / safe * (1.0 - jnp.exp(-safe / (4.0 * screen_omega * screen_omega)))
    return jnp.where(gsquare > 0, values, math.pi / (screen_omega * screen_omega))


def real_basis(count):
    half = count // 2
    freq = np.array(list(range(half + 1)) + list(range(1, count - half)))
    angle = 2.0 * np.pi * (np.arange(count)[:, None] * freq[None, :] % count) / count
    table = np.where(np.arange(count)[None, :] <= half, np.cos(angle), np.sin(angle))
    table = table / np.sqrt((table**2).sum(axis=0, keepdims=True))
    return table.astype(np.float32), freq.astype(np.float32)


MESH = pl.DeviceIdType.MESH


def rounded(value, unit):
    return -(-value // unit) * unit


def high_low(table):
    high = table.astype(jnp.bfloat16)
    low = (table - high.astype(np.float32)).astype(jnp.bfloat16)
    return high, low


def right_table(table, lanes):
    count = table.shape[0]
    high, low = high_low(table)
    out = np.zeros((2 * lanes, 2 * lanes), jnp.bfloat16)
    out[:count, :count] = high
    out[lanes : lanes + count, :count] = high
    out[:count, lanes : lanes + count] = low
    return out


def left_table(table):
    return np.concatenate(high_low(table), axis=0)


def split(values):
    high = values.astype(jnp.bfloat16)
    low = (values - high.astype(jnp.float32)).astype(jnp.bfloat16)
    return jnp.concatenate([high, low], axis=-1)


def from_right(values, table):
    lanes = values.shape[-1]
    out = jnp.dot(split(values), table, preferred_element_type=jnp.float32)
    return out[:, :lanes] + out[:, lanes:]


def from_left(table, values):
    count, lanes = values.shape
    out = jnp.dot(table, split(values), preferred_element_type=jnp.float32)
    return out[:count, :lanes] + (out[:count, lanes:] + out[count:, :lanes])


def exchange_kernel(
    nband, nplane, lines, early,
    psi_ref, filter_ref, right_fwd_ref, right_inv_ref, left_fwd_ref, left_inv_ref, out_ref,
    src_ref, send_ref, full_ref, back_ref,
    spread_send, spread_recv, own_sem, fwd_send, fwd_recv, fwd_own, back_send, back_recv, back_own,
):
    me = lax.axis_index("band")
    here = lax.axis_index("plane")
    mine = lax.rem(me, SOURCES)
    partner = me + 1 - 2 * mine
    above = lax.rem(me + 2, nband)
    below = lax.rem(me + nband - 2, nband)
    thick, count, lanes = psi_ref.shape
    padded = full_ref.shape[1]

    barrier = pltpu.get_barrier_semaphore()
    for other in (partner, above, below):
        pl.semaphore_signal(barrier, inc=1, device_id={"band": other}, device_id_type=MESH)
    for step in range(1, nplane):
        pl.semaphore_signal(
            barrier, inc=1, device_id={"plane": lax.rem(here + step, nplane)}, device_id_type=MESH
        )
    pl.semaphore_wait(barrier, 2 + nplane)

    def own(c):
        return pltpu.make_async_copy(psi_ref.at[c], src_ref.at[mine, c], own_sem.at[c])

    def spread(kind, which, c, target):
        return pltpu.make_async_remote_copy(
            src_ref=src_ref.at[which, c],
            dst_ref=src_ref.at[which, c],
            send_sem=spread_send.at[kind, c],
            recv_sem=spread_recv.at[kind, c],
            device_id={"band": target},
            device_id_type=MESH,
        )

    def forward(step, c):
        target = lax.rem(here + step, nplane)
        return pltpu.make_async_remote_copy(
            src_ref=send_ref.at[c, target],
            dst_ref=full_ref.at[here * thick + c],
            send_sem=fwd_send.at[step - 1, c],
            recv_sem=fwd_recv.at[step - 1, c],
            device_id={"plane": target},
            device_id_type=MESH,
        )

    def forward_own(c):
        return pltpu.make_async_copy(
            send_ref.at[c, here], full_ref.at[here * thick + c], fwd_own.at[c]
        )

    def back_parts(c, target):
        if c is None:
            planes, rows = pl.ds(0, thick), pl.ds(0, early)
            source = full_ref.at[pl.ds(target * thick, thick), rows]
            return source, back_ref.at[planes, here, rows], thick
        rows = pl.ds(early, padded - early)
        return full_ref.at[target * thick + c, rows], back_ref.at[c, here, rows], c

    def backward(step, c):
        target = lax.rem(here + step, nplane)
        source, landing, slot = back_parts(c, target)
        return pltpu.make_async_remote_copy(
            src_ref=source,
            dst_ref=landing,
            send_sem=back_send.at[step - 1, slot],
            recv_sem=back_recv.at[step - 1, slot],
            device_id={"plane": target},
            device_id_type=MESH,
        )

    def backward_own(c):
        source, landing, slot = back_parts(c, here)
        return pltpu.make_async_copy(source, landing, back_own.at[slot])

    @pl.when(me < SOURCES)
    def _():
        @pl.loop(0, thick)
        def _(c):
            own(c).start()

    @pl.loop(0, thick)
    def _(c):
        @pl.when(me < SOURCES)
        def _():
            own(c).wait()

        @pl.when(me >= SOURCES)
        def _():
            spread(0, mine, c, above).wait_recv()

        @pl.when(me + 2 < nband)
        def _():
            spread(0, mine, c, above).start()

        spread(1, mine, c, partner).start()
        spread(1, 1 - mine, c, partner).wait_recv()

        psi = psi_ref[c]
        density = jnp.concatenate([psi * src_ref[j, c] for j in range(SOURCES)], axis=0)
        half = from_right(density, right_fwd_ref[...])
        whole = jnp.concatenate(
            [
                from_left(left_fwd_ref[...], half[j * count : (j + 1) * count])
                for j in range(SOURCES)
            ],
            axis=0,
        )
        for p in range(nplane):
            send_ref[c, p, 0:lines] = whole[p * lines : (p + 1) * lines]
        for step in range(1, nplane):
            forward(step, c).start()
        forward_own(c).start()

    @pl.loop(0, thick)
    def _(c):
        for step in range(1, nplane):
            forward(step, c).wait_recv()
        forward_own(c).wait()

    rows_ref = full_ref.reshape(nplane * thick * padded, lanes)

    def filtered(r):
        where = (pl.ds(r, count, stride=padded), slice(None))
        spectrum = from_left(left_fwd_ref[...], rows_ref[where]) * filter_ref[r]
        rows_ref[where] = from_left(left_inv_ref[...], spectrum)

    def filter_rows(start, stop):
        unroll = 4 if (stop - start) % 4 == 0 else 2 if (stop - start) % 2 == 0 else 1

        @pl.loop(0, (stop - start) // unroll)
        def _(t):
            for u in range(unroll):
                filtered(start + t * unroll + u)

    if early:
        filter_rows(0, early)
        for step in range(1, nplane):
            backward(step, None).start()
        backward_own(None).start()
    filter_rows(early, lines)

    @pl.loop(0, thick)
    def _(c):
        for step in range(1, nplane):
            backward(step, c).start()
        backward_own(c).start()

    if early:
        for step in range(1, nplane):
            backward(step, None).wait_recv()
        backward_own(None).wait()

    @pl.loop(0, thick)
    def _(c):
        for step in range(1, nplane):
            backward(step, c).wait_recv()
        backward_own(c).wait()
        whole = jnp.concatenate([back_ref[c, p, 0:lines] for p in range(nplane)], axis=0)
        half = jnp.concatenate(
            [
                from_left(left_inv_ref[...], whole[j * count : (j + 1) * count])
                for j in range(SOURCES)
            ],
            axis=0,
        )
        potential = from_right(half, right_inv_ref[...])
        total = src_ref[0, c] * potential[:count]
        for j in range(1, SOURCES):
            total = total + src_ref[j, c] * potential[j * count : (j + 1) * count]
        out_ref[c] = -mixing * total

    @pl.loop(0, thick)
    def _(c):
        spread(1, mine, c, partner).wait_send()

        @pl.when(me + 2 < nband)
        def _():
            spread(0, mine, c, above).wait_send()

        for step in range(1, nplane):
            forward(step, c).wait_send()
            backward(step, c).wait_send()

    if early:
        for step in range(1, nplane):
            backward(step, None).wait_send()


def on_device(orbitals):
    nband = lax.axis_size("band")
    nplane = lax.axis_size("plane")
    rows, thick, flat = orbitals.shape
    count = thick * nplane
    lanes = rounded(count, 128)
    lines = SOURCES * count // nplane
    padded = rounded(lines, 8)
    early = 16 if padded >= 32 else 8 if padded >= 16 else 0
    table, freq = real_basis(count)
    freq = jnp.asarray(freq)
    local = orbitals.reshape(thick, count, count)
    local = jnp.pad(local, ((0, 0), (0, 0), (0, lanes - count)))
    line = lax.axis_index("plane") * lines + jnp.arange(lines, dtype=jnp.int32)
    freq_mine = jnp.take(freq, line % count)
    freq_last = jnp.pad(freq, (0, lanes - count))
    filters = kernel_values(
        freq_mine[:, None, None] ** 2 + freq[None, :, None] ** 2 + freq_last[None, None, :] ** 2
    )
    tables = (
        right_table(table, lanes),
        right_table(table.T, lanes),
        left_table(table.T),
        left_table(table),
    )
    dma = pltpu.SemaphoreType.DMA
    vmem = pl.BlockSpec(memory_space=pltpu.VMEM)
    out = pl.pallas_call(
        functools.partial(exchange_kernel, nband, nplane, lines, early),
        out_shape=jax.ShapeDtypeStruct((thick, count, lanes), jnp.float32),
        in_specs=[vmem] * 6,
        out_specs=vmem,
        scratch_shapes=[
            pltpu.VMEM((SOURCES, thick, count, lanes), jnp.float32),
            pltpu.VMEM((thick, nplane, padded, lanes), jnp.float32),
            pltpu.VMEM((count, padded, lanes), jnp.float32),
            pltpu.VMEM((thick, nplane, padded, lanes), jnp.float32),
            dma((2, thick)),
            dma((2, thick)),
            dma((thick,)),
            dma((nplane - 1, thick)),
            dma((nplane - 1, thick)),
            dma((thick,)),
            dma((nplane - 1, thick + 1)),
            dma((nplane - 1, thick + 1)),
            dma((thick + 1,)),
        ],
        compiler_params=pltpu.CompilerParams(
            collective_id=0, has_side_effects=True, vmem_limit_bytes=48 * 2**20
        ),
        name="exchange",
    )(local, filters, *[jnp.asarray(t) for t in tables])
    return out[:, :, :count].reshape(rows, thick, flat)


def solution(mesh):
    placed = (P("band", "plane", None),)
    return jax.shard_map(
        on_device, mesh=mesh, in_specs=placed, out_specs=P("band", "plane", None), check_vma=False
    )
```

time: 189 us -> 184 us (0.974)
  Pallas kernels: 54 us -> 169 us
  waiting for transfers between devices: 57.2 us -> 0 us
  matrix products: 23.7 us -> 0 us
  starting transfers between devices: 21.9 us -> 0 us
  local copies, waits for them, and re-layouts: 25.8 us -> 6.47 us
  other arithmetic: 5.45 us -> 8.52 us
    pallas_call x1, Pallas kernels: 54 us -> 169 us  [on_device(): pl.pallas_call(functools.partial(exchange_kernel, nband, nplane, lines, e...]
    all_to_all x4 -> x0, waiting for transfers between devices: 57.2 us -> none  [the longest x2 29.8 us: on_device(): lax.all_to_all(spectrum, 'plane', split_axis=1, concat_axis=0, tiled=True)]
    dot_general x12 -> x0, matrix products: 23.7 us -> none  [along(): return jnp.einsum(spec, values, table, precision=high)]
    all_to_all x4 -> x0, starting transfers between devices: 21.9 us -> none  [the longest x2 12 us: on_device(): lax.all_to_all(spectrum, 'plane', split_axis=1, concat_axis=0, tiled=True)]
    all_to_all x6 -> x0, local copies, waits for them, and re-layouts: 9.38 us -> none  [the longest x4 6.01 us: on_device(): lax.all_to_all(back, 'plane', split_axis=0, concat_axis=1, tiled=True)]
    dot_general x4 -> x0, local copies, waits for them, and re-layouts: 5.06 us -> none  [along(): return jnp.einsum(spec, values, table, precision=high)]
    transpose x2 -> x0, local copies, waits for them, and re-layouts: 4.58 us -> none  [along(): return jnp.einsum(spec, values, table, precision=high)]
    select_n x0 -> x2, other arithmetic: none -> 3.05 us  [the longest x1 3.03 us: kernel_values(): jnp.where(gsquare > 0, values, math.pi / (screen_omega * screen_omega))]
  transfers between devices with their start and end apart: 4 -> 0, of which waited for: 4 -> 0; matrix products, arithmetic and copies ran while one was open for 15% -> 0% of each run, Pallas kernels for 0% -> 0%
where the time goes in v1:
time: 184 us
  Pallas kernels  169 us (92%)
  other arithmetic  8.52 us (5%)
  local copies, waits for them, and re-layouts  6.47 us (4%)
    pallas_call x1, Pallas kernels, on_device(): pl.pallas_call(functools.partial(exchange_kernel, nband, nplane, lines, e...  169 us
    unnamed x1, other arithmetic  4.71 us

profile of v1, /device:TPU:25, one launch (start us, length us, event | category | flops | bytes accessed | tf_op | source)
XLA Modules:
  0.0 184.1 jit_solution(8834270199308697101)
XLA Ops:
  0.0 1.4 gather_fusion
  1.5 0.7 broadcast_add_fusion
  2.2 4.7 %reduce = f32[28,12544]{1,0:T(8,128)S(1)} reduce(f32[1,28,12544]{2,0,1:T(1,128)} %param.6, f32[]{:T(128)} %constant.71), dimensions={0}, to_apply=%param.6.reduce_sub_computation | reduce | bytes 2809860 | tf_op args[0]
  6.9 0.0 copy-start.4
  6.9 1.4 reshape.100
  8.4 0.0 copy-start
  8.4 0.0 copy-start.1
  8.4 0.0 copy-start.2
  8.4 0.0 copy-start.3
  8.4 0.1 pad.8.psi_ref
  8.5 0.0 copy-done.4
  8.5 3.0 %compare_select_fusion.filter_ref = f32[56,112,128]{2,1,0:T(8,128)} fusion(f32[128]{0:T(128)S(1)} %copy-done.4, f32[56,112]{1,0:T(8,128)S(1)} %broadcast_add_fusion), kind=kLoop, calls=%fused_computation.1 | loop fusion | flops 8028160 | bytes 3236864 | tf_op jit(solution)/shard_map/jit(_where)/select_n | solution.py:23
  11.6 0.0 copy-done
  11.6 0.0 copy-done.1
  11.6 0.0 copy-done.2
  11.6 0.0 copy-done.3
  11.6 169.0 %exchange.1 = f32[28,112,128]{2,1,0:T(8,128)S(1)} custom-call(f32[28,112,128]{2,1,0:T(8,128)S(1)} %pad.8.psi_ref, f32[56,112,128]{2,1,0:T(8,128)} %compare_select_fusion.filter_ref, bf16[256,256]{1,0:T(8,128)(2,1)S(1)} %copy-done.1, bf16[256,256]{1,0:T(8,128)(2,1)S(1)} %copy-done, bf16[224,112]{1,0:T(8,128)(2,1)S(1)} %copy-done.3, bf16[224,112]{1,0:T(8,128)(2,1)S(1)} %copy-done.2), custom_call_target="tpu_custom_call" | custom-call | tf_op jit(solution)/shard_map/exchange/pallas_call | solution.py:298
  180.6 3.5 %reshape.110 = f32[1,28,12544]{2,0,1:T(1,128)} reshape(f32[28,112,112]{2,1,0:T(8,128)S(1)} %bitcast.3) | data formatting | bytes 2809856 | tf_op jit(solution)/shard_map/reshape | solution.py:323
  (3 shorter events, 0.0 us)
Async XLA Ops:
  6.9 1.6 copy-start.4
  8.4 3.2 %copy-start = (bf16[256,256]{1,0:T(8,128)(2,1)S(1)}, bf16[256,256]{1,0:T(8,128)(2,1)}, u32[]{:S(2)}) copy-start(bf16[256,256]{1,0:T(8,128)(2,1)} %constant.60.clone.right_inv_ref) | copy-start | bytes 393220
  8.4 3.2 %copy-start.1 = (bf16[256,256]{1,0:T(8,128)(2,1)S(1)}, bf16[256,256]{1,0:T(8,128)(2,1)}, u32[]{:S(2)}) copy-start(bf16[256,256]{1,0:T(8,128)(2,1)} %constant.59.clone.right_fwd_ref) | copy-start | bytes 393220
  8.4 3.2 %copy-start.2 = (bf16[224,112]{1,0:T(8,128)(2,1)S(1)}, bf16[224,112]{1,0:T(8,128)(2,1)}, u32[]{:S(2)}) copy-start(bf16[224,112]{1,0:T(8,128)(2,1)} %constant.62.clone.left_inv_ref) | copy-start | bytes 150532
  8.4 3.2 %copy-start.3 = (bf16[224,112]{1,0:T(8,128)(2,1)S(1)}, bf16[224,112]{1,0:T(8,128)(2,1)}, u32[]{:S(2)}) copy-start(bf16[224,112]{1,0:T(8,128)(2,1)} %constant.61.clone.left_fwd_ref) | copy-start | bytes 150532

commit v2 on v1

--- a/solution.py
+++ b/solution.py
@@ -10,6 +10,7 @@
 from jax.sharding import PartitionSpec as P
 
 SOURCES = 2
+AHEAD = 4
 
 screen_omega = 0.106
 cell_length = 46.93
@@ -104,9 +105,9 @@
     def own(c):
         return pltpu.make_async_copy(psi_ref.at[c], src_ref.at[mine, c], own_sem.at[c])
 
-    def spread(kind, which, c, target):
+    def spread(kind, which, c, target, first=False):
         return pltpu.make_async_remote_copy(
-            src_ref=src_ref.at[which, c],
+            src_ref=psi_ref.at[c] if first else src_ref.at[which, c],
             dst_ref=src_ref.at[which, c],
             send_sem=spread_send.at[kind, c],
             recv_sem=spread_recv.at[kind, c],
@@ -158,23 +159,35 @@
     def _():
         @pl.loop(0, thick)
         def _(c):
+            spread(0, mine, c, above, True).start()
+            spread(1, mine, c, partner, True).start()
             own(c).start()
 
-    @pl.loop(0, thick)
-    def _(c):
+    def relay(c):
+        @pl.when(me >= SOURCES)
+        def _():
+            spread(0, mine, c, above).wait_recv()
+
+            @pl.when(me + 2 < nband)
+            def _():
+                spread(0, mine, c, above).start()
+
+            spread(1, mine, c, partner).start()
+
+    ahead = min(AHEAD, thick)
+    for c in range(ahead):
+        relay(c)
+
+    @pl.loop(0, thick)
+    def _(c):
+        @pl.when(c + ahead < thick)
+        def _():
+            relay(c + ahead)
+
         @pl.when(me < SOURCES)
         def _():
             own(c).wait()
 
-        @pl.when(me >= SOURCES)
-        def _():
-            spread(0, mine, c, above).wait_recv()
-
-        @pl.when(me + 2 < nband)
-        def _():
-            spread(0, mine, c, above).start()
-
-        spread(1, mine, c, partner).start()
         spread(1, 1 - mine, c, partner).wait_recv()
 
         psi = psi_ref[c]

time: 184 us -> 114 us (0.62)
  Pallas kernels: 169 us -> 98.6 us
    pallas_call x1, Pallas kernels: 169 us -> 98.6 us  [on_device(): pl.pallas_call(functools.partial(exchange_kernel, nband, nplane, lines, e...]
where the time goes in v2:
time: 114 us
  Pallas kernels  98.6 us (86%)
  other arithmetic  8.52 us (7%)
  local copies, waits for them, and re-layouts  6.47 us (6%)
    pallas_call x1, Pallas kernels, on_device(): pl.pallas_call(functools.partial(exchange_kernel, nband, nplane, lines, e...  98.6 us
    unnamed x1, other arithmetic  4.71 us
    reshape x1, local copies, waits for them, and re-layouts, on_device(): return out[:, :, :count].reshape(rows, thick, flat)  3.49 us
    select_n x1, other arithmetic, kernel_values(): jnp.where(gsquare > 0, values, math.pi / (screen_omega * screen_omega))  3.03 us

profile of v2, /device:TPU:25, one launch (start us, length us, event | category | flops | bytes accessed | tf_op | source)
XLA Modules:
  0.0 113.7 jit_solution(7619918174091818543)
XLA Ops:
  0.0 1.4 %gather_fusion = f32[56]{0:T(128)S(1)} fusion(f32[112]{0:T(128)} %constant.58.clone, s32[1024]{0:T(1024)S(1)} %pad_clamp_fusion), kind=kCustom, calls=%fused_computation | custom fusion | bytes 672 | tf_op jit(solution)/shard_map/jit(_take)/gather | solution.py:298
  1.5 0.7 broadcast_add_fusion
  2.2 4.7 %reduce = f32[28,12544]{1,0:T(8,128)S(1)} reduce(f32[1,28,12544]{2,0,1:T(1,128)} %param.6, f32[]{:T(128)} %constant.71), dimensions={0}, to_apply=%param.6.reduce_sub_computation | reduce | bytes 2809860 | tf_op args[0]
  6.9 0.0 copy-start.4
  6.9 1.4 %reshape.100 = f32[28,112,112]{2,1,0:T(8,128)S(1)} reshape(f32[28,12544]{1,0:T(8,128)S(1)} %reduce) | data formatting | bytes 2809856 | tf_op jit(solution)/shard_map/reshape | solution.py:295
  8.4 0.0 copy-start
  8.4 0.0 copy-start.1
  8.4 0.0 copy-start.2
  8.4 0.0 copy-start.3
  8.4 0.1 pad.8.psi_ref
  8.5 0.0 copy-done.4
  8.5 3.0 %compare_select_fusion.filter_ref = f32[56,112,128]{2,1,0:T(8,128)} fusion(f32[128]{0:T(128)S(1)} %copy-done.4, f32[56,112]{1,0:T(8,128)S(1)} %broadcast_add_fusion), kind=kLoop, calls=%fused_computation.1 | loop fusion | flops 8028160 | bytes 3236864 | tf_op jit(solution)/shard_map/jit(_where)/select_n | solution.py:24
  11.6 0.0 copy-done
  11.6 0.0 copy-done.1
  11.6 0.0 copy-done.2
  11.6 0.0 copy-done.3
  11.6 98.6 %exchange.1 = f32[28,112,128]{2,1,0:T(8,128)S(1)} custom-call(f32[28,112,128]{2,1,0:T(8,128)S(1)} %pad.8.psi_ref, f32[56,112,128]{2,1,0:T(8,128)} %compare_select_fusion.filter_ref, bf16[256,256]{1,0:T(8,128)(2,1)S(1)} %copy-done.1, bf16[256,256]{1,0:T(8,128)(2,1)S(1)} %copy-done, bf16[224,112]{1,0:T(8,128)(2,1)S(1)} %copy-done.3, bf16[224,112]{1,0:T(8,128)(2,1)S(1)} %copy-done.2), custom_call_target="tpu_custom_call" | custom-call | tf_op jit(solution)/shard_map/exchange/pallas_call | solution.py:311
  110.2 3.5 %reshape.110 = f32[1,28,12544]{2,0,1:T(1,128)} reshape(f32[28,112,112]{2,1,0:T(8,128)S(1)} %bitcast.3) | data formatting | bytes 2809856 | tf_op jit(solution)/shard_map/reshape | solution.py:336
  (3 shorter events, 0.0 us)
Async XLA Ops:
  6.9 1.6 %copy-start.4 = (f32[128]{0:T(128)S(1)}, f32[128]{0:T(128)}, u32[]{:S(2)}) copy-start(f32[128]{0:T(128)} %constant.70) | copy-start | bytes 1540
  8.4 3.2 %copy-start = (bf16[256,256]{1,0:T(8,128)(2,1)S(1)}, bf16[256,256]{1,0:T(8,128)(2,1)}, u32[]{:S(2)}) copy-start(bf16[256,256]{1,0:T(8,128)(2,1)} %constant.60.clone.right_inv_ref) | copy-start | bytes 393220
  8.4 3.2 %copy-start.1 = (bf16[256,256]{1,0:T(8,128)(2,1)S(1)}, bf16[256,256]{1,0:T(8,128)(2,1)}, u32[]{:S(2)}) copy-start(bf16[256,256]{1,0:T(8,128)(2,1)} %constant.59.clone.right_fwd_ref) | copy-start | bytes 393220
  8.4 3.2 %copy-start.2 = (bf16[224,112]{1,0:T(8,128)(2,1)S(1)}, bf16[224,112]{1,0:T(8,128)(2,1)}, u32[]{:S(2)}) copy-start(bf16[224,112]{1,0:T(8,128)(2,1)} %constant.62.clone.left_inv_ref) | copy-start | bytes 150532
  8.4 3.2 %copy-start.3 = (bf16[224,112]{1,0:T(8,128)(2,1)S(1)}, bf16[224,112]{1,0:T(8,128)(2,1)}, u32[]{:S(2)}) copy-start(bf16[224,112]{1,0:T(8,128)(2,1)} %constant.61.clone.left_fwd_ref) | copy-start | bytes 150532

commit v3 on v2

--- a/solution.py
+++ b/solution.py
@@ -78,10 +78,15 @@
     return out[:count, :lanes] + (out[:count, lanes:] + out[count:, :lanes])
 
 
+def run_offsets(count):
+    runs = 128 // math.gcd(count, 128)
+    return runs, [divmod(u * count, 128) for u in range(runs)]
+
+
 def exchange_kernel(
     nband, nplane, lines, early,
-    psi_ref, filter_ref, right_fwd_ref, right_inv_ref, left_fwd_ref, left_inv_ref, out_ref,
-    src_ref, send_ref, full_ref, back_ref,
+    flat_ref, right_fwd_ref, right_inv_ref, left_fwd_ref, left_inv_ref, out_ref,
+    psi_ref, filter_ref, src_ref, send_ref, full_ref, back_ref,
     spread_send, spread_recv, own_sem, fwd_send, fwd_recv, fwd_own, back_send, back_recv, back_own,
 ):
     me = lax.axis_index("band")
@@ -93,6 +98,12 @@
     thick, count, lanes = psi_ref.shape
     padded = full_ref.shape[1]
 
+    runs, offsets = run_offsets(count)
+    psi_rows = psi_ref.reshape(thick * count, lanes)
+
+    def psi_at(y):
+        return (pl.ds(y, thick, stride=count), slice(None))
+
     barrier = pltpu.get_barrier_semaphore()
     for other in (partner, above, below):
         pl.semaphore_signal(barrier, inc=1, device_id={"band": other}, device_id_type=MESH)
@@ -100,6 +111,16 @@
         pl.semaphore_signal(
             barrier, inc=1, device_id={"plane": lax.rem(here + step, nplane)}, device_id_type=MESH
         )
+
+    @pl.loop(0, count // runs)
+    def _(t):
+        block = flat_ref[:, pl.ds(pl.multiple_of(t * runs * count, 128), runs * count)]
+        for u, (tile, shift) in enumerate(offsets):
+            wide = block[:, tile * 128 : min((tile + 2) * 128, runs * count)]
+            if shift:
+                wide = pltpu.roll(wide, wide.shape[1] - shift, 1)
+            psi_rows[psi_at(t * runs + u)] = wide[:, :lanes]
+
     pl.semaphore_wait(barrier, 2 + nplane)
 
     def own(c):
@@ -163,6 +184,21 @@
             spread(1, mine, c, partner, True).start()
             own(c).start()
 
+    half_count = count // 2
+
+    def squared(index):
+        wave = jnp.where(index <= half_count, index, index - half_count)
+        return wave * wave
+
+    plane_squares = squared(lax.broadcasted_iota(jnp.int32, (count, lanes), 0)) + squared(
+        lax.broadcasted_iota(jnp.int32, (count, lanes), 1)
+    )
+
+    @pl.loop(0, lines)
+    def _(r):
+        row = squared(lax.rem(here * lines + r, count))
+        filter_ref[r] = kernel_values((plane_squares + row).astype(jnp.float32))
+
     def relay(c):
         @pl.when(me >= SOURCES)
         def _():
@@ -212,6 +248,14 @@
             forward(step, c).wait_recv()
         forward_own(c).wait()
 
+    @pl.loop(0, thick)
+    def _(c):
+        spread(1, mine, c, partner).wait_send()
+
+        @pl.when(me + 2 < nband)
+        def _():
+            spread(0, mine, c, above).wait_send()
+
     rows_ref = full_ref.reshape(nplane * thick * padded, lanes)
 
     def filtered(r):
@@ -262,16 +306,10 @@
         total = src_ref[0, c] * potential[:count]
         for j in range(1, SOURCES):
             total = total + src_ref[j, c] * potential[j * count : (j + 1) * count]
-        out_ref[c] = -mixing * total
-
-    @pl.loop(0, thick)
-    def _(c):
-        spread(1, mine, c, partner).wait_send()
-
-        @pl.when(me + 2 < nband)
-        def _():
-            spread(0, mine, c, above).wait_send()
-
+        psi_ref[c] = -mixing * total
+
+    @pl.loop(0, thick)
+    def _(c):
         for step in range(1, nplane):
             forward(step, c).wait_send()
             backward(step, c).wait_send()
@@ -279,6 +317,25 @@
     if early:
         for step in range(1, nplane):
             backward(step, None).wait_send()
+
+    @pl.loop(0, count // runs)
+    def _(t):
+        tiles = [None] * (runs * count // 128)
+        for u, (tile, shift) in enumerate(offsets):
+            value = psi_rows[psi_at(t * runs + u)]
+            if not shift:
+                parts = [value]
+            else:
+                wide = jnp.concatenate([value, jnp.zeros_like(value)], axis=1)
+                wide = pltpu.roll(wide, shift, 1)
+                parts = [wide[:, :128], wide[:, 128:]]
+            for k, piece in enumerate(parts):
+                if tile + k < len(tiles):
+                    old = tiles[tile + k]
+                    tiles[tile + k] = piece if old is None else old + piece
+        out_ref[:, pl.ds(pl.multiple_of(t * runs * count, 128), runs * count)] = jnp.concatenate(
+            tiles, axis=1
+        )
 
 
 def on_device(orbitals):
@@ -290,16 +347,7 @@
     lines = SOURCES * count // nplane
     padded = rounded(lines, 8)
     early = 16 if padded >= 32 else 8 if padded >= 16 else 0
-    table, freq = real_basis(count)
-    freq = jnp.asarray(freq)
-    local = orbitals.reshape(thick, count, count)
-    local = jnp.pad(local, ((0, 0), (0, 0), (0, lanes - count)))
-    line = lax.axis_index("plane") * lines + jnp.arange(lines, dtype=jnp.int32)
-    freq_mine = jnp.take(freq, line % count)
-    freq_last = jnp.pad(freq, (0, lanes - count))
-    filters = kernel_values(
-        freq_mine[:, None, None] ** 2 + freq[None, :, None] ** 2 + freq_last[None, None, :] ** 2
-    )
+    table, _ = real_basis(count)
     tables = (
         right_table(table, lanes),
         right_table(table.T, lanes),
@@ -310,10 +358,12 @@
     vmem = pl.BlockSpec(memory_space=pltpu.VMEM)
     out = pl.pallas_call(
         functools.partial(exchange_kernel, nband, nplane, lines, early),
-        out_shape=jax.ShapeDtypeStruct((thick, count, lanes), jnp.float32),
-        in_specs=[vmem] * 6,
+        out_shape=jax.ShapeDtypeStruct((thick, flat), jnp.float32),
+        in_specs=[vmem] * 5,
         out_specs=vmem,
         scratch_shapes=[
+            pltpu.VMEM((thick, count, lanes), jnp.float32),
+            pltpu.VMEM((lines, count, lanes), jnp.float32),
             pltpu.VMEM((SOURCES, thick, count, lanes), jnp.float32),
             pltpu.VMEM((thick, nplane, padded, lanes), jnp.float32),
             pltpu.VMEM((count, padded, lanes), jnp.float32),
@@ -332,8 +382,8 @@
             collective_id=0, has_side_effects=True, vmem_limit_bytes=48 * 2**20
         ),
         name="exchange",
-    )(local, filters, *[jnp.asarray(t) for t in tables])
-    return out[:, :, :count].reshape(rows, thick, flat)
+    )(orbitals.reshape(thick, flat), *[jnp.asarray(t) for t in tables])
+    return out.reshape(rows, thick, flat)
 
 
 def solution(mesh):

time: 114 us -> 103 us (0.904)
  other arithmetic: 8.52 us -> 0 us
  local copies, waits for them, and re-layouts: 6.47 us -> 4.07 us
    unnamed x1 -> x0, other arithmetic: 4.71 us -> none
    select_n x2 -> x0, other arithmetic: 3.05 us -> none  [the longest x1 3.03 us: kernel_values(): jnp.where(gsquare > 0, values, math.pi / (screen_omega * screen_omega))]
    reshape x2 -> x1, local copies, waits for them, and re-layouts: 4.9 us -> 2.53 us  [on_device(): return out.reshape(rows, thick, flat)]
    unnamed x10 -> x9, local copies, waits for them, and re-layouts: 0.03 us -> 1.53 us
    gather x1 -> x0, local copies, waits for them, and re-layouts: 1.43 us -> none  [on_device(): freq_mine = jnp.take(freq, line % count)]
where the time goes in v3:
time: 103 us
  Pallas kernels  98.4 us (96%)
  local copies, waits for them, and re-layouts  4.07 us (4%)
    pallas_call x1, Pallas kernels, on_device(): pl.pallas_call(functools.partial(exchange_kernel, nband, nplane, lines, e...  98.4 us
    reshape x1, local copies, waits for them, and re-layouts, on_device(): return out.reshape(rows, thick, flat)  2.53 us

profile of v3, /device:TPU:25, one launch (start us, length us, event | category | flops | bytes accessed | tf_op | source)
XLA Modules:
  0.0 102.5 jit_solution(3491085129863954070)
XLA Ops:
  0.0 0.0 copy-start.2
  0.0 0.0 copy-start.3
  0.0 0.0 copy-start
  0.0 0.0 copy-start.1
  0.0 1.5 %copy.9 = f32[1,28,12544]{2,1,0:T(8,128)S(1)} copy(f32[1,28,12544]{2,0,1:T(1,128)} %param.5) | data formatting | bytes 2809856
  1.5 0.0 copy-done.2
  1.6 0.0 copy-done.3
  1.6 0.0 copy-done
  1.6 0.0 copy-done.1
  1.6 98.4 %exchange.1 = f32[28,12544]{1,0:T(8,128)S(1)} custom-call(f32[28,12544]{1,0:T(8,128)S(1)} %bitcast.5, bf16[256,256]{1,0:T(8,128)(2,1)S(1)} %copy-done.1, bf16[256,256]{1,0:T(8,128)(2,1)S(1)} %copy-done, bf16[224,112]{1,0:T(8,128)(2,1)S(1)} %copy-done.3, bf16[224,112]{1,0:T(8,128)(2,1)S(1)} %copy-done.2), custom_call_target="tpu_custom_call" | custom-call | tf_op jit(solution)/shard_map/exchange/pallas_call | solution.py:359
  100.0 2.5 %copy.6 = f32[1,28,12544]{2,0,1:T(1,128)} copy(f32[1,28,12544]{2,1,0:T(8,128)S(1)} %bitcast.4) | data formatting | bytes 2809856 | tf_op jit(solution)/shard_map/reshape | solution.py:386
Async XLA Ops:
  0.0 1.5 %copy-start.2 = (bf16[224,112]{1,0:T(8,128)(2,1)S(1)}, bf16[224,112]{1,0:T(8,128)(2,1)}, u32[]{:S(2)}) copy-start(bf16[224,112]{1,0:T(8,128)(2,1)} %constant.11.clone.left_inv_ref) | copy-start | bytes 150532
  0.0 1.5 %copy-start.3 = (bf16[224,112]{1,0:T(8,128)(2,1)S(1)}, bf16[224,112]{1,0:T(8,128)(2,1)}, u32[]{:S(2)}) copy-start(bf16[224,112]{1,0:T(8,128)(2,1)} %constant.10.clone.left_fwd_ref) | copy-start | bytes 150532
  0.0 1.6 %copy-start = (bf16[256,256]{1,0:T(8,128)(2,1)S(1)}, bf16[256,256]{1,0:T(8,128)(2,1)}, u32[]{:S(2)}) copy-start(bf16[256,256]{1,0:T(8,128)(2,1)} %constant.9.clone.right_inv_ref) | copy-start | bytes 393220
  0.0 1.6 %copy-start.1 = (bf16[256,256]{1,0:T(8,128)(2,1)S(1)}, bf16[256,256]{1,0:T(8,128)(2,1)}, u32[]{:S(2)}) copy-start(bf16[256,256]{1,0:T(8,128)(2,1)} %constant.8.clone.right_fwd_ref) | copy-start | bytes 393220

commit v4 on v3

--- a/solution.py
+++ b/solution.py
@@ -10,7 +10,7 @@
 from jax.sharding import PartitionSpec as P
 
 SOURCES = 2
-AHEAD = 4
+AHEAD = 2
 
 screen_omega = 0.106
 cell_length = 46.93
@@ -346,7 +346,7 @@
     lanes = rounded(count, 128)
     lines = SOURCES * count // nplane
     padded = rounded(lines, 8)
-    early = 16 if padded >= 32 else 8 if padded >= 16 else 0
+    early = 8 if padded >= 16 else 0
     table, _ = real_basis(count)
     tables = (
         right_table(table, lanes),

time: 103 us -> 106 us (1.029)
  Pallas kernels: 98.4 us -> 101 us
    pallas_call x1, Pallas kernels: 98.4 us -> 101 us  [on_device(): pl.pallas_call(functools.partial(exchange_kernel, nband, nplane, lines, e...]
where the time goes in v4:
time: 106 us
  Pallas kernels  101 us (95%)
  local copies, waits for them, and re-layouts  4.07 us (4%)
    pallas_call x1, Pallas kernels, on_device(): pl.pallas_call(functools.partial(exchange_kernel, nband, nplane, lines, e...  101 us
    reshape x1, local copies, waits for them, and re-layouts, on_device(): return out.reshape(rows, thick, flat)  2.53 us

profile of v4, /device:TPU:25, one launch (start us, length us, event | category | flops | bytes accessed | tf_op | source)
XLA Modules:
  0.0 105.6 jit_solution(8800226592782574835)
XLA Ops:
  0.0 0.0 copy-start.2
  0.0 0.0 copy-start.3
  0.0 0.0 copy-start
  0.0 0.0 copy-start.1
  0.0 1.5 %copy.9 = f32[1,28,12544]{2,1,0:T(8,128)S(1)} copy(f32[1,28,12544]{2,0,1:T(1,128)} %param.5) | data formatting | bytes 2809856
  1.5 0.0 copy-done.2
  1.6 0.0 copy-done.3
  1.6 0.0 copy-done
  1.6 0.0 copy-done.1
  1.6 101.5 %exchange.1 = f32[28,12544]{1,0:T(8,128)S(1)} custom-call(f32[28,12544]{1,0:T(8,128)S(1)} %bitcast.5, bf16[256,256]{1,0:T(8,128)(2,1)S(1)} %copy-done.1, bf16[256,256]{1,0:T(8,128)(2,1)S(1)} %copy-done, bf16[224,112]{1,0:T(8,128)(2,1)S(1)} %copy-done.3, bf16[224,112]{1,0:T(8,128)(2,1)S(1)} %copy-done.2), custom_call_target="tpu_custom_call" | custom-call | tf_op jit(solution)/shard_map/exchange/pallas_call | solution.py:359
  103.1 2.5 %copy.6 = f32[1,28,12544]{2,0,1:T(1,128)} copy(f32[1,28,12544]{2,1,0:T(8,128)S(1)} %bitcast.4) | data formatting | bytes 2809856 | tf_op jit(solution)/shard_map/reshape | solution.py:386
Async XLA Ops:
  0.0 1.5 %copy-start.2 = (bf16[224,112]{1,0:T(8,128)(2,1)S(1)}, bf16[224,112]{1,0:T(8,128)(2,1)}, u32[]{:S(2)}) copy-start(bf16[224,112]{1,0:T(8,128)(2,1)} %constant.11.clone.left_inv_ref) | copy-start | bytes 150532
  0.0 1.5 %copy-start.3 = (bf16[224,112]{1,0:T(8,128)(2,1)S(1)}, bf16[224,112]{1,0:T(8,128)(2,1)}, u32[]{:S(2)}) copy-start(bf16[224,112]{1,0:T(8,128)(2,1)} %constant.10.clone.left_fwd_ref) | copy-start | bytes 150532
  0.0 1.6 %copy-start = (bf16[256,256]{1,0:T(8,128)(2,1)S(1)}, bf16[256,256]{1,0:T(8,128)(2,1)}, u32[]{:S(2)}) copy-start(bf16[256,256]{1,0:T(8,128)(2,1)} %constant.9.clone.right_inv_ref) | copy-start | bytes 393220
  0.0 1.6 %copy-start.1 = (bf16[256,256]{1,0:T(8,128)(2,1)S(1)}, bf16[256,256]{1,0:T(8,128)(2,1)}, u32[]{:S(2)}) copy-start(bf16[256,256]{1,0:T(8,128)(2,1)} %constant.8.clone.right_fwd_ref) | copy-start | bytes 393220
